TPU v7x, 32 devices: a whole 2x2x4 slice. The times are simulated.
32 devices in a mesh: grp: 4 (over y, core), rep: 8 (over z, x).
Axes of the slice: x: 2, y: 2, z: 4, core: 2. Of those that a mesh axis runs over, the one named last changes fastest.
Arguments:
- embeddings: bfloat16 [16384, 768], P(('grp', 'rep')), may hold values from -6 to 6
- cluster_ids: int32 [16384], P(('grp', 'rep')), may hold values from 0 to 12287, as said below
- owner_bounds: int32 [32], replicated, may hold values from 0 to 12287, as said below
Outputs:
- distance: float32 [16384], P(('grp', 'rep'))
- slot_index: int32 [16384], P(('grp', 'rep'))
- centroids: bfloat16 [32, 576, 768], P(('grp', 'rep'))
Inputs may be any that keep to these rules, and one draw needn't show every extreme that they name: `cluster_ids`: in the rows of one device at most 48 rows belong to the clusters of one owner (owner o holds clusters owner_bounds[o] up to the next bound); in every draw some owner gets exactly 48 rows from every device. `owner_bounds`: owners are ordered grp first, then rep. The bounds rise from 0; each owner holds from 192 to 576 clusters, the last owner ending at 12288; some owner holds exactly 576.
All inputs are finite; a program needn't handle non-finite values.
Results may differ from a plain program's by a relative error of at most 0.004.
Values may be sent and summed in bfloat16 or wider, within the bound.
No kernel may reach another device: no remote copies, remote signals or barrier semaphores. Data moves between devices by JAX's collectives and lax.ppermute only.
A program may use at most 128 MiB of HBM per device.

v0:
```python
import jax
import jax.numpy as jnp
from jax import lax
from jax.sharding import PartitionSpec as P

CL_DEV = 384


epsilon = 1e-06
norm_floor = 0.25


def entering(part, axis, combine, identity):
    place = lax.axis_index(axis)
    gathered = lax.all_gather(part, axis)
    state = jnp.zeros_like(part) + jnp.asarray(identity, part.dtype)

    def one(hop, state):
        return combine(state, lax.dynamic_index_in_dim(gathered, hop, 0, False))

    return lax.fori_loop(0, place, one, state)


def shards(embeddings, cluster_ids, owner_bounds):
    groups = lax.axis_size("grp")
    replicas = lax.axis_size("rep")
    owner_total = groups * replicas
    position = lax.axis_index("grp") * replicas + lax.axis_index("rep")
    row_count = embeddings.shape[0]
    feature_count = embeddings.shape[1]
    clusters = CL_DEV * owner_total
    slot_count = 3 * row_count // owner_total
    owner_limit = CL_DEV + CL_DEV // 2
    row_range = jnp.arange(row_count, dtype=jnp.int32)
    owner_of = jnp.sum(owner_bounds[None, :] <= cluster_ids[:, None], axis=1, dtype=jnp.int32) - 1
    order = jnp.argsort(cluster_ids, stable=True)
    sorted_place = jnp.zeros((row_count,), jnp.int32).at[order].set(row_range)
    sorted_owner = owner_of[order]
    same_owner = sorted_place - jnp.searchsorted(sorted_owner, owner_of, side="left")
    target = owner_of * slot_count + same_owner
    counts = jnp.zeros((clusters,), jnp.int32).at[cluster_ids].add(1)
    before = entering(counts, ("grp", "rep"), jnp.add, jnp.zeros_like(counts))
    sorted_ids = cluster_ids[order]
    same_cluster = sorted_place - jnp.searchsorted(sorted_ids, cluster_ids, side="left")
    local_slot = before[cluster_ids] + same_cluster
    values = embeddings.astype(jnp.float32)
    unit_rows = (
        values * lax.rsqrt(jnp.sum(values * values, axis=1, keepdims=True) + epsilon)
    ).astype(jnp.bfloat16)
    send_rows = (
        jnp.zeros((owner_total * slot_count, feature_count), jnp.bfloat16).at[target].set(unit_rows)
    )
    send_ids = jnp.full((owner_total * slot_count,), -1, jnp.int32).at[target].set(cluster_ids)
    got_rows, got_ids = (
        lax.all_to_all(
            send_rows.reshape(owner_total, slot_count, feature_count),
            ("grp", "rep"),
            split_axis=0,
            concat_axis=0,
            tiled=True,
        ),
        lax.all_to_all(
            send_ids.reshape(owner_total, slot_count),
            ("grp", "rep"),
            split_axis=0,
            concat_axis=0,
            tiled=True,
        ),
    )
    flat_rows = got_rows.reshape(owner_total * slot_count, feature_count)
    flat_ids = got_ids.reshape(-1)
    local_index = flat_ids - owner_bounds[position]
    membership = jnp.arange(owner_limit)[:, None] == local_index[None, :]
    member_sums = jnp.dot(
        membership.astype(jnp.bfloat16), flat_rows, preferred_element_type=jnp.float32
    )
    members = jnp.sum(membership, axis=1, dtype=jnp.float32)
    centroid = member_sums / jnp.maximum(members, 1.0)[:, None]
    centroid_norm = jnp.sqrt(jnp.sum(centroid * centroid, axis=1))
    unit_centroid = (centroid / jnp.maximum(centroid_norm, norm_floor)[:, None]).astype(
        jnp.bfloat16
    )
    picked = unit_centroid[jnp.clip(local_index, 0, owner_limit - 1)]
    owner_distance = 1.0 - jnp.einsum(
        "rd,rd->r", flat_rows, picked, preferred_element_type=jnp.float32
    )
    returned = lax.all_to_all(
        owner_distance.reshape(owner_total, slot_count),
        ("grp", "rep"),
        split_axis=0,
        concat_axis=0,
        tiled=True,
    )
    distance = returned.reshape(-1)[target]
    return (distance, local_slot, unit_centroid[None])


def solution(mesh):
    placed = (P(("grp", "rep"), None), P(("grp", "rep")), P())
    return jax.shard_map(
        shards,
        mesh=mesh,
        in_specs=placed,
        out_specs=(P(("grp", "rep")), P(("grp", "rep")), P(("grp", "rep"), None, None)),
        check_vma=False,
    )
```

profile of v0, /device:TPU:0, one launch (start us, length us, event | category | flops | bytes accessed | tf_op | source)
XLA Modules:
  0.0 216.7 jit_solution(953403876074517466)
XLA Ops:
  7.9 3.8 %scatter_custom_fusion.3 = s32[12288]{0:T(1024)} fusion(s32[512]{0:T(512)S(1)} %compare_select_fusion.1, s32[512]{0:T(512)S(1)} %broadcast.93, s32[]{:T(128)} %constant.81.clone.1), kind=kCustom, calls=%fused_computation.37 | custom fusion | flops 512 | bytes 49156 | tf_op jit(solution)/shard_map/scatter-add | solution.py:41
  11.8 4.4 %sort.17 = (s32[512]{0:T(512)}, s32[512]{0:T(512)S(1)}) sort(s32[512]{0:T(512)} %param.10, s32[512]{0:T(512)S(1)} %iota.11), dimensions={0}, to_apply=%region_1.0 | sort | flops 4608 | bytes 8192 | tf_op jit(solution)/shard_map/jit(argsort)/sort | solution.py:36
  17.0 3.6 %gather_fusion.6 = s32[512]{0:T(512)S(1)} fusion(s32[512]{0:T(512)} %param.10, s32[1024]{0:T(1024)S(1)} %pad_clamp_fusion.5), kind=kCustom, calls=%fused_computation.6 | custom fusion | bytes 6144 | tf_op jit(solution)/shard_map/gather | solution.py:43
  20.7 3.5 %gather_fusion.2 = s32[512]{0:T(512)S(1)} fusion(s32[512]{0:T(512)S(1)} %broadcast_add_fusion, s32[1024]{0:T(1024)S(1)} %pad_clamp_fusion.5), kind=kCustom, calls=%fused_computation.2 | custom fusion | bytes 6144 | tf_op jit(solution)/shard_map/gather | solution.py:38
  24.2 35.9 %while.48 = (s32[]{:T(128)}, u32[512]{0:T(512)S(1)}, u32[512]{0:T(512)S(1)}, s32[512]{0:T(512)S(1)}, s32[512]{0:T(512)S(1)}, /*index=5*/s32[]{:T(128)}, s32[]{:T(128)}, s32[]{}) while((s32[]{:T(128)}, u32[512]{0:T(512)S(1)}, u32[512]{0:T(512)S(1)}, s32[512]{0:T(512)S(1)}, s32[512]{0:T(512)S(1)}, /*index=5*/s32[]{:T(128)}, ...), condition=%wide.region_4.5_spmd.clone, body=%wide.region_3.4_spmd.clone.sunk | while | flops 10244 | bytes 40045 | solution.py:39
  24.2 3.5 %gather_fusion = s32[512]{0:T(512)S(1)} fusion(s32[512]{0:T(512)S(1)} %get-tuple-element.385, u32[1024]{0:T(1024)S(1)} %pad_clamp_fusion.8), kind=kCustom, calls=%fused_computation.clone.clone.1 | custom fusion | bytes 6144 | tf_op jit(solution)/shard_map/jit(searchsorted)/jit(_searchsorted_scan_impl)/vmap(jit(_searchsorted_scan_impl))/while/body/eval_jaxpr/gather | solution.py:39
  27.8 3.5 %gather_fusion = s32[512]{0:T(512)S(1)} fusion(s32[512]{0:T(512)S(1)} %get-tuple-element.385, u32[1024]{0:T(1024)S(1)} %pad_clamp_fusion.8), kind=kCustom, calls=%fused_computation.clone.clone.1 | custom fusion | bytes 6144 | tf_op jit(solution)/shard_map/jit(searchsorted)/jit(_searchsorted_scan_impl)/vmap(jit(_searchsorted_scan_impl))/while/body/eval_jaxpr/gather | solution.py:39
  31.4 3.5 %gather_fusion = s32[512]{0:T(512)S(1)} fusion(s32[512]{0:T(512)S(1)} %get-tuple-element.385, u32[1024]{0:T(1024)S(1)} %pad_clamp_fusion.8), kind=kCustom, calls=%fused_computation.clone.clone.1 | custom fusion | bytes 6144 | tf_op jit(solution)/shard_map/jit(searchsorted)/jit(_searchsorted_scan_impl)/vmap(jit(_searchsorted_scan_impl))/while/body/eval_jaxpr/gather | solution.py:39
  35.0 3.5 %gather_fusion = s32[512]{0:T(512)S(1)} fusion(s32[512]{0:T(512)S(1)} %get-tuple-element.385, u32[1024]{0:T(1024)S(1)} %pad_clamp_fusion.8), kind=kCustom, calls=%fused_computation.clone.clone.1 | custom fusion | bytes 6144 | tf_op jit(solution)/shard_map/jit(searchsorted)/jit(_searchsorted_scan_impl)/vmap(jit(_searchsorted_scan_impl))/while/body/eval_jaxpr/gather | solution.py:39
  38.6 3.5 %gather_fusion = s32[512]{0:T(512)S(1)} fusion(s32[512]{0:T(512)S(1)} %get-tuple-element.385, u32[1024]{0:T(1024)S(1)} %pad_clamp_fusion.8), kind=kCustom, calls=%fused_computation.clone.clone.1 | custom fusion | bytes 6144 | tf_op jit(solution)/shard_map/jit(searchsorted)/jit(_searchsorted_scan_impl)/vmap(jit(_searchsorted_scan_impl))/while/body/eval_jaxpr/gather | solution.py:39
  42.2 3.5 %gather_fusion = s32[512]{0:T(512)S(1)} fusion(s32[512]{0:T(512)S(1)} %get-tuple-element.385, u32[1024]{0:T(1024)S(1)} %pad_clamp_fusion.8), kind=kCustom, calls=%fused_computation.clone.clone.1 | custom fusion | bytes 6144 | tf_op jit(solution)/shard_map/jit(searchsorted)/jit(_searchsorted_scan_impl)/vmap(jit(_searchsorted_scan_impl))/while/body/eval_jaxpr/gather | solution.py:39
  45.7 3.5 %gather_fusion = s32[512]{0:T(512)S(1)} fusion(s32[512]{0:T(512)S(1)} %get-tuple-element.385, u32[1024]{0:T(1024)S(1)} %pad_clamp_fusion.8), kind=kCustom, calls=%fused_computation.clone.clone.1 | custom fusion | bytes 6144 | tf_op jit(solution)/shard_map/jit(searchsorted)/jit(_searchsorted_scan_impl)/vmap(jit(_searchsorted_scan_impl))/while/body/eval_jaxpr/gather | solution.py:39
  49.3 3.5 %gather_fusion = s32[512]{0:T(512)S(1)} fusion(s32[512]{0:T(512)S(1)} %get-tuple-element.385, u32[1024]{0:T(1024)S(1)} %pad_clamp_fusion.8), kind=kCustom, calls=%fused_computation.clone.clone.1 | custom fusion | bytes 6144 | tf_op jit(solution)/shard_map/jit(searchsorted)/jit(_searchsorted_scan_impl)/vmap(jit(_searchsorted_scan_impl))/while/body/eval_jaxpr/gather | solution.py:39
  52.9 3.5 %gather_fusion = s32[512]{0:T(512)S(1)} fusion(s32[512]{0:T(512)S(1)} %get-tuple-element.385, u32[1024]{0:T(1024)S(1)} %pad_clamp_fusion.8), kind=kCustom, calls=%fused_computation.clone.clone.1 | custom fusion | bytes 6144 | tf_op jit(solution)/shard_map/jit(searchsorted)/jit(_searchsorted_scan_impl)/vmap(jit(_searchsorted_scan_impl))/while/body/eval_jaxpr/gather | solution.py:39
  56.5 3.5 %gather_fusion = s32[512]{0:T(512)S(1)} fusion(s32[512]{0:T(512)S(1)} %get-tuple-element.385, u32[1024]{0:T(1024)S(1)} %pad_clamp_fusion.8), kind=kCustom, calls=%fused_computation.clone.clone.1 | custom fusion | bytes 6144 | tf_op jit(solution)/shard_map/jit(searchsorted)/jit(_searchsorted_scan_impl)/vmap(jit(_searchsorted_scan_impl))/while/body/eval_jaxpr/gather | solution.py:39
  60.1 35.9 %while.49 = (s32[]{:T(128)}, u32[512]{0:T(512)S(1)}, u32[512]{0:T(512)S(1)}, s32[512]{0:T(512)S(1)}, s32[512]{0:T(512)S(1)}, /*index=5*/s32[]{:T(128)}, s32[]{:T(128)}, s32[]{}) while((s32[]{:T(128)}, u32[512]{0:T(512)S(1)}, u32[512]{0:T(512)S(1)}, s32[512]{0:T(512)S(1)}, s32[512]{0:T(512)S(1)}, /*index=5*/s32[]{:T(128)}, ...), condition=%wide.region_14.15_spmd.clone, body=%wide.region_13.14_spmd.clone.sunk | while | flops 10244 | bytes 40045 | solution.py:44
  60.1 3.5 %gather_fusion.1 = s32[512]{0:T(512)S(1)} fusion(s32[512]{0:T(512)S(1)} %get-tuple-element.361, u32[1024]{0:T(1024)S(1)} %pad_clamp_fusion.9), kind=kCustom, calls=%fused_computation.1.clone.clone.1 | custom fusion | bytes 6144 | tf_op jit(solution)/shard_map/jit(searchsorted)/jit(_searchsorted_scan_impl)/vmap(jit(_searchsorted_scan_impl))/while/body/eval_jaxpr/gather | solution.py:39
  63.7 3.5 %gather_fusion.1 = s32[512]{0:T(512)S(1)} fusion(s32[512]{0:T(512)S(1)} %get-tuple-element.361, u32[1024]{0:T(1024)S(1)} %pad_clamp_fusion.9), kind=kCustom, calls=%fused_computation.1.clone.clone.1 | custom fusion | bytes 6144 | tf_op jit(solution)/shard_map/jit(searchsorted)/jit(_searchsorted_scan_impl)/vmap(jit(_searchsorted_scan_impl))/while/body/eval_jaxpr/gather | solution.py:39
  67.3 3.5 %gather_fusion.1 = s32[512]{0:T(512)S(1)} fusion(s32[512]{0:T(512)S(1)} %get-tuple-element.361, u32[1024]{0:T(1024)S(1)} %pad_clamp_fusion.9), kind=kCustom, calls=%fused_computation.1.clone.clone.1 | custom fusion | bytes 6144 | tf_op jit(solution)/shard_map/jit(searchsorted)/jit(_searchsorted_scan_impl)/vmap(jit(_searchsorted_scan_impl))/while/body/eval_jaxpr/gather | solution.py:39
  70.9 3.5 %gather_fusion.1 = s32[512]{0:T(512)S(1)} fusion(s32[512]{0:T(512)S(1)} %get-tuple-element.361, u32[1024]{0:T(1024)S(1)} %pad_clamp_fusion.9), kind=kCustom, calls=%fused_computation.1.clone.clone.1 | custom fusion | bytes 6144 | tf_op jit(solution)/shard_map/jit(searchsorted)/jit(_searchsorted_scan_impl)/vmap(jit(_searchsorted_scan_impl))/while/body/eval_jaxpr/gather | solution.py:39
  74.5 3.5 %gather_fusion.1 = s32[512]{0:T(512)S(1)} fusion(s32[512]{0:T(512)S(1)} %get-tuple-element.361, u32[1024]{0:T(1024)S(1)} %pad_clamp_fusion.9), kind=kCustom, calls=%fused_computation.1.clone.clone.1 | custom fusion | bytes 6144 | tf_op jit(solution)/shard_map/jit(searchsorted)/jit(_searchsorted_scan_impl)/vmap(jit(_searchsorted_scan_impl))/while/body/eval_jaxpr/gather | solution.py:39
  78.1 3.5 %gather_fusion.1 = s32[512]{0:T(512)S(1)} fusion(s32[512]{0:T(512)S(1)} %get-tuple-element.361, u32[1024]{0:T(1024)S(1)} %pad_clamp_fusion.9), kind=kCustom, calls=%fused_computation.1.clone.clone.1 | custom fusion | bytes 6144 | tf_op jit(solution)/shard_map/jit(searchsorted)/jit(_searchsorted_scan_impl)/vmap(jit(_searchsorted_scan_impl))/while/body/eval_jaxpr/gather | solution.py:39
  81.7 3.5 %gather_fusion.1 = s32[512]{0:T(512)S(1)} fusion(s32[512]{0:T(512)S(1)} %get-tuple-element.361, u32[1024]{0:T(1024)S(1)} %pad_clamp_fusion.9), kind=kCustom, calls=%fused_computation.1.clone.clone.1 | custom fusion | bytes 6144 | tf_op jit(solution)/shard_map/jit(searchsorted)/jit(_searchsorted_scan_impl)/vmap(jit(_searchsorted_scan_impl))/while/body/eval_jaxpr/gather | solution.py:39
  85.2 3.5 %gather_fusion.1 = s32[512]{0:T(512)S(1)} fusion(s32[512]{0:T(512)S(1)} %get-tuple-element.361, u32[1024]{0:T(1024)S(1)} %pad_clamp_fusion.9), kind=kCustom, calls=%fused_computation.1.clone.clone.1 | custom fusion | bytes 6144 | tf_op jit(solution)/shard_map/jit(searchsorted)/jit(_searchsorted_scan_impl)/vmap(jit(_searchsorted_scan_impl))/while/body/eval_jaxpr/gather | solution.py:39
  88.8 3.5 %gather_fusion.1 = s32[512]{0:T(512)S(1)} fusion(s32[512]{0:T(512)S(1)} %get-tuple-element.361, u32[1024]{0:T(1024)S(1)} %pad_clamp_fusion.9), kind=kCustom, calls=%fused_computation.1.clone.clone.1 | custom fusion | bytes 6144 | tf_op jit(solution)/shard_map/jit(searchsorted)/jit(_searchsorted_scan_impl)/vmap(jit(_searchsorted_scan_impl))/while/body/eval_jaxpr/gather | solution.py:39
  92.4 3.5 %gather_fusion.1 = s32[512]{0:T(512)S(1)} fusion(s32[512]{0:T(512)S(1)} %get-tuple-element.361, u32[1024]{0:T(1024)S(1)} %pad_clamp_fusion.9), kind=kCustom, calls=%fused_computation.1.clone.clone.1 | custom fusion | bytes 6144 | tf_op jit(solution)/shard_map/jit(searchsorted)/jit(_searchsorted_scan_impl)/vmap(jit(_searchsorted_scan_impl))/while/body/eval_jaxpr/gather | solution.py:39
  107.3 9.6 %all-to-all-start.1 = ((s32[32,1,48]{2,1,0:T(1,128)}), s32[32,1,48]{2,1,0:T(1,128)S(1)}, u32[]{:S(2)}, u32[]{:S(2)}) async-start(s32[32,1,48]{2,1,0:T(1,128)} %all_to_all.16), calls=%async_computation.1 | async-start | bytes 32768 | tf_op jit(solution)/shard_map/all_to_all | solution.py:62
  116.9 4.4 %scatter_custom_fusion.1 = bf16[1536,768]{1,0:T(8,128)(2,1)} fusion(s32[512]{0:T(512)S(1)} %get-tuple-element.222, bf16[]{:T(256)} %constant.80.clone.1, bf16[512,768]{1,0:T(8,128)(2,1)S(1)} %copy-done.3, f32[512]{0:T(512)S(1)} %add_rsqrt_fusion), kind=kCustom, calls=%fused_computation.32 | custom fusion | flops 1179648 | bytes 3147778 | tf_op jit(solution)/shard_map/scatter | solution.py:51
  129.3 53.4 %all-to-all-done = bf16[32,48,768]{2,1,0:T(8,128)(2,1)S(1)} async-done(((bf16[32,48,768]{2,1,0:T(8,128)(2,1)}), bf16[32,48,768]{2,1,0:T(8,128)(2,1)S(1)}, u32[]{:S(2)}, u32[]{:S(2)}) %all-to-all-start) | async-done | bytes 2359328 | tf_op jit(solution)/shard_map/all_to_all | solution.py:55
  185.9 5.0 %gather_fusion.3 = bf16[1536,768]{1,0:T(8,128)(2,1)S(1)} fusion(bf16[576,768]{1,0:T(8,128)(2,1)S(1)} %divide_convert_fusion, s32[2048]{0:T(1024)S(1)} %pad_clamp_fusion.2), kind=kCustom, calls=%fused_computation.3 | custom fusion | bytes 4724736 | tf_op jit(solution)/shard_map/gather | solution.py:83
  199.7 4.6 %all-to-all-done.2 = f32[32,1,48]{2,1,0:T(1,128)S(1)} async-done(((f32[32,1,48]{2,1,0:T(1,128)}), f32[32,1,48]{2,1,0:T(1,128)S(1)}, u32[]{:S(2)}, u32[]{:S(2)}) %all-to-all-start.2) | async-done | bytes 6176 | tf_op jit(solution)/shard_map/all_to_all | solution.py:87
  205.6 4.3 %gather_fusion.4 = f32[512]{0:T(512)} fusion(f32[1536]{0:T(1024)S(1)} %reshape.78, s32[1024]{0:T(1024)S(1)} %pad_clamp_fusion.4), kind=kCustom, calls=%fused_computation.4 | custom fusion | bytes 6144 | tf_op jit(solution)/shard_map/gather | solution.py:94
  (158 shorter events, 34.8 us)
Async XLA Ops:
  7.2 91.6 %all-gather.3.cloned.1.call-start = ((), (), s32[]{:S(2)}) async-start(), calls=%async_computation.3 | async-start | bytes 1622016 | tf_op jit(solution)/shard_map/all_gather | solution.py:15
  24.2 35.9 %copy-start = (s32[512]{0:T(512)S(1)}, s32[512]{0:T(512)}, u32[]{:S(2)}) copy-start(s32[512]{0:T(512)} %param.10) | copy-start | bytes 6148
  60.1 38.4 %copy-start.3 = (bf16[512,768]{1,0:T(8,128)(2,1)S(1)}, bf16[512,768]{1,0:T(8,128)(2,1)}, u32[]{:S(2)}) copy-start(bf16[512,768]{1,0:T(8,128)(2,1)} %param.9) | copy-start | bytes 2359300
  107.3 16.7 %all-to-all-start.1 = ((s32[32,1,48]{2,1,0:T(1,128)}), s32[32,1,48]{2,1,0:T(1,128)S(1)}, u32[]{:S(2)}, u32[]{:S(2)}) async-start(s32[32,1,48]{2,1,0:T(1,128)} %all_to_all.16), calls=%async_computation.1 | async-start | bytes 32768 | tf_op jit(solution)/shard_map/all_to_all | solution.py:62
  124.0 3.3 %copy-start.4 = (s32[32]{0:T(128)S(1)}, s32[32]{0:T(128)}, u32[]{:S(2)}) copy-start(s32[32]{0:T(128)} %param.11) | copy-start | bytes 388
  124.0 58.8 %all-to-all-start = ((bf16[32,48,768]{2,1,0:T(8,128)(2,1)}), bf16[32,48,768]{2,1,0:T(8,128)(2,1)S(1)}, u32[]{:S(2)}, u32[]{:S(2)}) async-start(bf16[32,48,768]{2,1,0:T(8,128)(2,1)} %bitcast.11), calls=%async_computation | async-start | bytes 4718592 | tf_op jit(solution)/shard_map/all_to_all | solution.py:55
  182.7 1.8 copy-start.1
  184.5 1.2 copy-start.2
  194.0 10.3 %all-to-all-start.2 = ((f32[32,1,48]{2,1,0:T(1,128)}), f32[32,1,48]{2,1,0:T(1,128)S(1)}, u32[]{:S(2)}, u32[]{:S(2)}) async-start(f32[32,1,48]{2,1,0:T(1,128)} %all_to_all.18), calls=%async_computation.2 | async-start | bytes 32768 | tf_op jit(solution)/shard_map/all_to_all | solution.py:87
Sparse Core Ops, SparseCore 0:
  11.9 57.7 all-gather.2
where the time goes:
time: 217 us
  local copies, waits for them, and re-layouts  99.8 us (46%)
  waiting for transfers between devices  60.7 us (28%)
  other arithmetic  22.9 us (11%)
  starting transfers between devices  16.1 us (7%)
  between operations  14.3 us (7%)
    gather x20, local copies, waits for them, and re-layouts, shards(): jnp.searchsorted(sorted_owner, owner_of, side='left')  69.8 us
    all_to_all x1, waiting for transfers between devices, shards(): lax.all_to_all(send_rows.reshape(owner_total, slot_count, feature_count),...  53.4 us
    all_to_all x1, starting transfers between devices, shards(): lax.all_to_all(send_ids.reshape(owner_total, slot_count), ('grp', 'rep'),...  9.63 us
    gather x1, local copies, waits for them, and re-layouts, shards(): picked = unit_centroid[jnp.clip(local_index, 0, owner_limit - 1)]  4.97 us
    all_to_all x1, waiting for transfers between devices, shards(): lax.all_to_all(owner_distance.reshape(owner_total, slot_count), ('grp', '...  4.57 us
    sort x1, other arithmetic, shards(): order = jnp.argsort(cluster_ids, stable=True)  4.45 us
    scatter x1, other arithmetic, shards(): jnp.zeros((owner_total * slot_count, feature_count), jnp.bfloat16)  4.36 us
  transfers between devices with their start and end apart: 4, of which 3 were waited for; matrix products, arithmetic and copies ran while one was open for 44% of the time, Pallas kernels for 0%

commit v1 on v0

v1 whole, which is shorter than its diff:
```python
import jax
import jax.numpy as jnp
from jax import lax
from jax.sharding import PartitionSpec as P

CL_DEV = 384


epsilon = 1e-06
norm_floor = 0.25
axes = ("grp", "rep")


def exchange(part):
    return lax.all_to_all(part, axes, split_axis=0, concat_axis=0, tiled=True)


def shards(embeddings, cluster_ids, owner_bounds):
    groups = lax.axis_size("grp")
    replicas = lax.axis_size("rep")
    owner_total = groups * replicas
    position = lax.axis_index("grp") * replicas + lax.axis_index("rep")
    row_count = embeddings.shape[0]
    feature_count = embeddings.shape[1]
    slot_count = 3 * row_count // owner_total
    owner_limit = CL_DEV + CL_DEV // 2
    places = owner_total * slot_count
    row_range = jnp.arange(row_count, dtype=jnp.int32)
    place_range = jnp.arange(places, dtype=jnp.int32)

    owner_of = jnp.sum(owner_bounds[None, :] <= cluster_ids[:, None], axis=1, dtype=jnp.int32) - 1
    earlier = (owner_of[:, None] == owner_of[None, :]) & (row_range[None, :] < row_range[:, None])
    target = owner_of * slot_count + jnp.sum(earlier, axis=1, dtype=jnp.int32)
    placed = place_range[:, None] == target[None, :]
    send_ids = jnp.sum(jnp.where(placed, cluster_ids[None, :] + 1, 0), axis=1, dtype=jnp.int32) - 1
    flat_ids = exchange(send_ids.reshape(owner_total, slot_count)).reshape(-1)

    values = embeddings.astype(jnp.float32)
    unit_rows = (
        values * lax.rsqrt(jnp.sum(values * values, axis=1, keepdims=True) + epsilon)
    ).astype(jnp.bfloat16)
    send_rows = jnp.dot(
        placed.astype(jnp.bfloat16), unit_rows, preferred_element_type=jnp.float32
    ).astype(jnp.bfloat16)
    flat_rows = exchange(send_rows.reshape(owner_total, slot_count, feature_count)).reshape(
        places, feature_count
    )

    twins = (flat_ids[:, None] == flat_ids[None, :]) & (place_range[None, :] < place_range[:, None])
    rank = jnp.sum(twins, axis=1, dtype=jnp.int32)
    local_index = flat_ids - owner_bounds[position]
    membership = jnp.arange(owner_limit, dtype=jnp.int32)[:, None] == local_index[None, :]
    members = jnp.sum(membership, axis=1, dtype=jnp.float32)
    member_sums = jnp.dot(
        membership.astype(jnp.bfloat16), flat_rows, preferred_element_type=jnp.float32
    )
    centroid = member_sums / jnp.maximum(members, 1.0)[:, None]
    centroid_norm = jnp.sqrt(jnp.sum(centroid * centroid, axis=1))
    unit_centroid = (centroid / jnp.maximum(centroid_norm, norm_floor)[:, None]).astype(
        jnp.bfloat16
    )
    products = lax.dot_general(
        unit_centroid, flat_rows, (((1,), (1,)), ((), ())), preferred_element_type=jnp.float32
    )
    owner_distance = 1.0 - jnp.sum(jnp.where(membership, products, 0.0), axis=0)
    answers = jnp.concatenate(
        [
            owner_distance.reshape(owner_total, slot_count),
            rank.astype(jnp.float32).reshape(owner_total, slot_count),
        ],
        axis=1,
    )
    returned = exchange(answers)
    mine = target[:, None] == place_range[None, :]
    distance = jnp.sum(jnp.where(mine, returned[:, :slot_count].reshape(1, -1), 0.0), axis=1)
    local_slot = jnp.sum(
        jnp.where(mine, returned[:, slot_count:].reshape(1, -1), 0.0), axis=1
    ).astype(jnp.int32)
    return (distance, local_slot, unit_centroid[None])


def solution(mesh):
    placed = (P(axes, None), P(axes), P())
    return jax.shard_map(
        shards,
        mesh=mesh,
        in_specs=placed,
        out_specs=(P(axes), P(axes), P(axes, None, None)),
        check_vma=False,
    )
```

time: 217 us -> 95.1 us (0.44)
  local copies, waits for them, and re-layouts: 99.8 us -> 2.25 us
  between operations: 14.3 us -> 0.75 us
  other arithmetic: 22.9 us -> 13.4 us
  matrix products: 1.78 us -> 7.53 us
  waiting for transfers between devices: 60.7 us -> 56 us
    gather x25 -> x0, local copies, waits for them, and re-layouts: 89.3 us -> none  [the longest x20 69.8 us: shards(): jnp.searchsorted(sorted_owner, owner_of, side='left')]
    dot_general x0 -> x2, matrix products: none -> 5.77 us  [the longest x1 4.14 us: shards(): jnp.dot(placed.astype(jnp.bfloat16), unit_rows, preferred_element_type=jn...]
    reduce_sum x0 -> x4, other arithmetic: none -> 4.93 us  [the longest x1 2.65 us: shards(): rank = jnp.sum(twins, axis=1, dtype=jnp.int32)]
    scatter x2 -> x0, local copies, waits for them, and re-layouts: 4.88 us -> none  [the longest x1 2.45 us: shards(): jnp.full((owner_total * slot_count,), -1, jnp.int32).at[target]]
    all_to_all x3, waiting for transfers between devices: 60.7 us -> 56 us  [exchange(): return lax.all_to_all(part, axes, split_axis=0, concat_axis=0, tiled=True)]
    sort x1 -> x0, other arithmetic: 4.45 us -> none  [shards(): order = jnp.argsort(cluster_ids, stable=True)]
    scatter x1 -> x0, other arithmetic: 4.36 us -> none  [shards(): jnp.zeros((owner_total * slot_count, feature_count), jnp.bfloat16)]
    scatter-add x1 -> x0, other arithmetic: 3.83 us -> none  [shards(): counts = jnp.zeros((clusters,), jnp.int32).at[cluster_ids].add(1)]
  transfers between devices with their start and end apart: 4 -> 3, of which waited for: 3 -> 3; matrix products, arithmetic and copies ran while one was open for 44% -> 15% of each run, Pallas kernels for 0% -> 0%
where the time goes in v1:
time: 95.1 us; the launch traced here: 94.7 us
  waiting for transfers between devices  56 us (59%)
  starting transfers between devices  14.7 us (15%)
  other arithmetic  13.4 us (14%)
  matrix products  7.53 us (8%)
  local copies, waits for them, and re-layouts  2.25 us (2%)
    all_to_all x3, waiting for transfers between devices, exchange(): return lax.all_to_all(part, axes, split_axis=0, concat_axis=0, tiled=True)  56 us
    all_to_all x3, starting transfers between devices, exchange(): return lax.all_to_all(part, axes, split_axis=0, concat_axis=0, tiled=True)  14.7 us
    dot_general x1, matrix products, shards(): jnp.dot(placed.astype(jnp.bfloat16), unit_rows, preferred_element_type=jn...  4.14 us
    reduce_sum x1, other arithmetic, shards(): rank = jnp.sum(twins, axis=1, dtype=jnp.int32)  2.65 us
    broadcast_in_dim x1, other arithmetic, shards(): return (distance, local_slot, unit_centroid[None])  2.56 us
  transfers between devices with their start and end apart: 3, of which 3 were waited for; matrix products, arithmetic and copies ran while one was open for 15% of the time, Pallas kernels for 0%

profile of v1, /device:TPU:0, one launch (start us, length us, event | category | flops | bytes accessed | tf_op | source)
XLA Modules:
  0.0 94.7 jit_solution(8862254501806167028)
XLA Ops:
  0.6 0.8 convert_reduce_fusion.3
  1.4 0.3 convert_reduce_fusion.2
  1.7 0.7 multiply_add_fusion
  2.4 0.4 select_reduce_fusion.3
  2.8 0.7 sub.33
  3.5 7.3 %all-to-all-start = ((s32[32,1,48]{2,1,0:T(1,128)}), s32[32,1,48]{2,1,0:T(1,128)S(1)}, u32[]{:S(2)}, u32[]{:S(2)}) async-start(s32[32,1,48]{2,1,0:T(1,128)} %sub.33), calls=%async_computation | async-start | bytes 32768 | tf_op jit(solution)/shard_map/all_to_all | solution.py:15
  10.8 1.4 %fusion.3 = f32[512]{0:T(512)S(1)} fusion(bf16[512,768]{1,0:T(8,128)(2,1)} %param.3), kind=kLoop, calls=%fused_computation.18 | loop fusion | flops 1179136 | bytes 788480 | tf_op jit(solution)/shard_map/reduce_sum | solution.py:40
  12.2 4.1 %convolution_convert_fusion = bf16[1536,768]{1,0:T(8,128)(2,1)} fusion(s32[512]{0:T(512)S(1)} %get-tuple-element.9, bf16[512,768]{1,0:T(8,128)(2,1)} %param.3, f32[512]{0:T(512)S(1)} %add_rsqrt_fusion), kind=kOutput, calls=%fused_computation.7 | convolution fusion | flops 1211105280 | bytes 3149824 | tf_op jit(solution)/shard_map/dot_general | solution.py:42
  16.3 1.6 %all-to-all-done = s32[32,1,48]{2,1,0:T(1,128)S(1)} async-done(((s32[32,1,48]{2,1,0:T(1,128)}), s32[32,1,48]{2,1,0:T(1,128)S(1)}, u32[]{:S(2)}, u32[]{:S(2)}) %all-to-all-start) | async-done | bytes 6176 | tf_op jit(solution)/shard_map/all_to_all | solution.py:15
  17.9 4.3 %all-to-all-start.1 = ((bf16[32,48,768]{2,1,0:T(8,128)(2,1)}), bf16[32,48,768]{2,1,0:T(8,128)(2,1)S(1)}, u32[]{:S(2)}, u32[]{:S(2)}) async-start(bf16[32,48,768]{2,1,0:T(8,128)(2,1)} %bitcast.12), calls=%async_computation.1 | async-start | bytes 4718592 | tf_op jit(solution)/shard_map/all_to_all | solution.py:15
  22.2 0.0 copy-done.1
  22.2 0.6 dynamic_slice.3
  22.8 0.5 broadcast.72
  23.3 0.7 reduce.3
  24.0 0.1 reshape.89
  24.1 2.6 %convert_reduce_fusion = s32[1536]{0:T(1024)S(1)} fusion(s32[1536]{0:T(1024)S(1)} %reshape.89), kind=kLoop, calls=%fused_computation | loop fusion | flops 11794944 | bytes 12288 | tf_op jit(solution)/shard_map/reduce_sum | solution.py:50
  26.7 0.1 convert_element_type.49
  26.8 0.7 broadcast_subtract_fusion
  27.4 0.4 convert_reduce_fusion.1
  27.9 49.9 %all-to-all-done.1 = bf16[32,48,768]{2,1,0:T(8,128)(2,1)S(1)} async-done(((bf16[32,48,768]{2,1,0:T(8,128)(2,1)}), bf16[32,48,768]{2,1,0:T(8,128)(2,1)S(1)}, u32[]{:S(2)}, u32[]{:S(2)}) %all-to-all-start.1) | async-done | bytes 2359328 | tf_op jit(solution)/shard_map/all_to_all | solution.py:15
  77.8 1.8 %multiply_reduce_fusion = (f32[576]{0:T(1024)S(1)}, f32[576,768]{1,0:T(8,128)S(1)}) fusion(f32[576]{0:T(1024)S(1)} %broadcast_maximum_fusion, bf16[1536,768]{1,0:T(8,128)(2,1)S(1)} %bitcast.10, s32[1536]{0:T(1024)S(1)} %broadcast_subtract_fusion), kind=kOutput, calls=%fused_computation.16 | convolution fusion | flops 1361165824 | bytes 4139520 | tf_op jit(solution)/shard_map/dot_general | solution.py:54
  79.6 1.6 %select_reduce_fusion = f32[1536]{0:T(1024)S(1)} fusion(bf16[1536,768]{1,0:T(8,128)(2,1)S(1)} %bitcast.11, s32[1536]{0:T(1024)S(1)} %broadcast_subtract_fusion, f32[576,768]{1,0:T(8,128)S(1)} %get-tuple-element.8, f32[576]{0:T(1024)S(1)} %maximum_multiply_fusion), kind=kOutput, calls=%fused_computation.3 | convolution fusion | flops 1362491904 | bytes 4143360 | tf_op jit(solution)/shard_map/dot_general | solution.py:62
  81.2 0.1 sub.37
  81.3 0.7 pad_maximum_fusion
  82.0 3.1 %all-to-all-start.2 = ((f32[32,1,96]{2,1,0:T(1,128)}), f32[32,1,96]{2,1,0:T(1,128)S(1)}, u32[]{:S(2)}, u32[]{:S(2)}) async-start(f32[32,1,96]{2,1,0:T(1,128)} %bitcast.3), calls=%async_computation.2 | async-start | bytes 32768 | tf_op jit(solution)/shard_map/all_to_all | solution.py:15
  85.1 2.6 %fusion.13 = bf16[1,576,768]{2,1,0:T(8,128)(2,1)} fusion(f32[576,768]{1,0:T(8,128)} %copy-done, f32[576]{0:T(1024)S(1)} %maximum_multiply_fusion), kind=kLoop, calls=%fused_computation.37 | loop fusion | flops 884736 | bytes 2656512 | tf_op jit(solution)/shard_map/broadcast_in_dim | solution.py:79
  87.7 4.6 %all-to-all-done.2 = f32[32,1,96]{2,1,0:T(1,128)S(1)} async-done(((f32[32,1,96]{2,1,0:T(1,128)}), f32[32,1,96]{2,1,0:T(1,128)S(1)}, u32[]{:S(2)}, u32[]{:S(2)}) %all-to-all-start.2) | async-done | bytes 12320 | tf_op jit(solution)/shard_map/all_to_all | solution.py:15
  92.2 0.1 fusion.9
  92.3 0.1 broadcast_in_dim.65
  92.4 0.1 broadcast_in_dim.62
  92.5 1.6 %select_reduce_fusion.1 = (f32[512]{0:T(512)S(1)}, f32[512]{0:T(512)}) fusion(f32[1536]{0:T(1024)S(1)} %broadcast_in_dim.65, s32[512]{0:T(512)S(1)} %get-tuple-element.9, f32[1536]{0:T(1024)S(1)} %broadcast_in_dim.62), kind=kLoop, calls=%fused_computation.8 | loop fusion | flops 3931136 | bytes 18432 | tf_op jit(solution)/shard_map/reduce_sum | solution.py:76
  94.1 0.6 convert_element_type.50
  (10 shorter events, 0.0 us)
Async XLA Ops:
  3.5 14.4 %all-to-all-start = ((s32[32,1,48]{2,1,0:T(1,128)}), s32[32,1,48]{2,1,0:T(1,128)S(1)}, u32[]{:S(2)}, u32[]{:S(2)}) async-start(s32[32,1,48]{2,1,0:T(1,128)} %sub.33), calls=%async_computation | async-start | bytes 32768 | tf_op jit(solution)/shard_map/all_to_all | solution.py:15
  17.9 4.3 %copy-start.1 = (s32[32]{0:T(128)S(1)}, s32[32]{0:T(128)}, u32[]{:S(2)}) copy-start(s32[32]{0:T(128)} %param.5) | copy-start | bytes 388
  17.9 59.9 %all-to-all-start.1 = ((bf16[32,48,768]{2,1,0:T(8,128)(2,1)}), bf16[32,48,768]{2,1,0:T(8,128)(2,1)S(1)}, u32[]{:S(2)}, u32[]{:S(2)}) async-start(bf16[32,48,768]{2,1,0:T(8,128)(2,1)} %bitcast.12), calls=%async_computation.1 | async-start | bytes 4718592 | tf_op jit(solution)/shard_map/all_to_all | solution.py:15
  79.5 1.7 %copy-start = (f32[576,768]{1,0:T(8,128)}, f32[576,768]{1,0:T(8,128)S(1)}, u32[]{:S(2)}) copy-start(f32[576,768]{1,0:T(8,128)S(1)} %get-tuple-element.8) | copy-start | bytes 5308420
  82.0 10.3 %all-to-all-start.2 = ((f32[32,1,96]{2,1,0:T(1,128)}), f32[32,1,96]{2,1,0:T(1,128)S(1)}, u32[]{:S(2)}, u32[]{:S(2)}) async-start(f32[32,1,96]{2,1,0:T(1,128)} %bitcast.3), calls=%async_computation.2 | async-start | bytes 32768 | tf_op jit(solution)/shard_map/all_to_all | solution.py:15

commit v2 on v1

--- a/solution.py
+++ b/solution.py
@@ -33,8 +33,6 @@
     target = owner_of * slot_count + jnp.sum(earlier, axis=1, dtype=jnp.int32)
     placed = place_range[:, None] == target[None, :]
     send_ids = jnp.sum(jnp.where(placed, cluster_ids[None, :] + 1, 0), axis=1, dtype=jnp.int32) - 1
-    flat_ids = exchange(send_ids.reshape(owner_total, slot_count)).reshape(-1)
-
     values = embeddings.astype(jnp.float32)
     unit_rows = (
         values * lax.rsqrt(jnp.sum(values * values, axis=1, keepdims=True) + epsilon)
@@ -42,9 +40,13 @@
     send_rows = jnp.dot(
         placed.astype(jnp.bfloat16), unit_rows, preferred_element_type=jnp.float32
     ).astype(jnp.bfloat16)
-    flat_rows = exchange(send_rows.reshape(owner_total, slot_count, feature_count)).reshape(
-        places, feature_count
-    )
+    send_rows, send_ids = lax.optimization_barrier((send_rows, send_ids))
+    with jax.named_scope("rows"):
+        flat_rows = exchange(send_rows.reshape(owner_total, slot_count, feature_count)).reshape(
+            places, feature_count
+        )
+    with jax.named_scope("ids"):
+        flat_ids = exchange(send_ids.reshape(owner_total, slot_count)).reshape(-1)
 
     twins = (flat_ids[:, None] == flat_ids[None, :]) & (place_range[None, :] < place_range[:, None])
     rank = jnp.sum(twins, axis=1, dtype=jnp.int32)

time: 95.1 us -> 98.6 us (1.037)
  blocking collectives: 0 us -> 14.3 us
  starting transfers between devices: 14.7 us -> 6.19 us
  waiting for transfers between devices: 56 us -> 54.5 us
    all_to_all x0 -> x1, blocking collectives: none -> 14.3 us  [exchange(): return lax.all_to_all(part, axes, split_axis=0, concat_axis=0, tiled=True)]
    all_to_all x3 -> x2, starting transfers between devices: 14.7 us -> 6.19 us  [exchange(): return lax.all_to_all(part, axes, split_axis=0, concat_axis=0, tiled=True)]
    all_to_all x3 -> x2, waiting for transfers between devices: 56 us -> 54.5 us  [exchange(): return lax.all_to_all(part, axes, split_axis=0, concat_axis=0, tiled=True)]
  transfers between devices with their start and end apart: 3 -> 2, of which waited for: 3 -> 2; matrix products, arithmetic and copies ran while one was open for 15% -> 8% of each run, Pallas kernels for 0% -> 0%
where the time goes in v2:
time: 98.6 us; the launch traced here: 98.2 us
  waiting for transfers between devices  54.5 us (55%)
  blocking collectives  14.3 us (15%)
  other arithmetic  13.4 us (14%)
  matrix products  7.54 us (8%)
  starting transfers between devices  6.19 us (6%)
  local copies, waits for them, and re-layouts  1.64 us (2%)
    all_to_all x2, waiting for transfers between devices, exchange(): return lax.all_to_all(part, axes, split_axis=0, concat_axis=0, tiled=True)  54.5 us
    all_to_all x1, blocking collectives, exchange(): return lax.all_to_all(part, axes, split_axis=0, concat_axis=0, tiled=True)  14.3 us
    all_to_all x2, starting transfers between devices, exchange(): return lax.all_to_all(part, axes, split_axis=0, concat_axis=0, tiled=True)  6.19 us
    dot_general x1, matrix products, shards(): jnp.dot(placed.astype(jnp.bfloat16), unit_rows, preferred_element_type=jn...  4.15 us
    reduce_sum x1, other arithmetic, shards(): rank = jnp.sum(twins, axis=1, dtype=jnp.int32)  2.65 us
    broadcast_in_dim x1, other arithmetic, shards(): return (distance, local_slot, unit_centroid[None])  2.56 us
  transfers between devices with their start and end apart: 2, of which 2 were waited for; matrix products, arithmetic and copies ran while one was open for 8% of the time, Pallas kernels for 0%

profile of v2, /device:TPU:0, one launch (start us, length us, event | category | flops | bytes accessed | tf_op | source)
XLA Modules:
  0.0 98.2 jit_solution(15079247601860223593)
XLA Ops:
  0.6 0.8 convert_reduce_fusion.3
  1.4 0.3 convert_reduce_fusion.2
  1.7 0.7 multiply_add_fusion
  2.4 1.4 %fusion.3 = f32[512]{0:T(512)S(1)} fusion(bf16[512,768]{1,0:T(8,128)(2,1)} %param.3), kind=kLoop, calls=%fused_computation.18 | loop fusion | flops 1179136 | bytes 788480 | tf_op jit(solution)/shard_map/reduce_sum | solution.py:38
  3.7 4.1 %convolution_convert_fusion = bf16[1536,768]{1,0:T(8,128)(2,1)} fusion(s32[512]{0:T(512)S(1)} %get-tuple-element.13, bf16[512,768]{1,0:T(8,128)(2,1)} %param.3, f32[512]{0:T(512)S(1)} %add_rsqrt_fusion), kind=kOutput, calls=%fused_computation.7 | convolution fusion | flops 1211105280 | bytes 3149824 | tf_op jit(solution)/shard_map/dot_general | solution.py:40
  7.9 0.4 select_reduce_fusion.3
  8.3 0.1 all_to_all.17
  8.4 14.3 %all_to_all.26 = s32[32,1,48]{2,1,0:T(1,128)S(1)} all-to-all(s32[32,1,48]{2,1,0:T(1,128)S(1)} %all_to_all.17), channel_id=1, replica_groups=mesh['grp'=4,'rep'=8] {'grp','rep'}, dimensions={0} | all-to-all | bytes 12288 | tf_op jit(solution)/shard_map/ids/all_to_all | solution.py:15
  22.7 2.9 %all-to-all-start.1 = ((bf16[32,48,768]{2,1,0:T(8,128)(2,1)}), bf16[32,48,768]{2,1,0:T(8,128)(2,1)S(1)}, u32[]{:S(2)}, u32[]{:S(2)}) async-start(bf16[32,48,768]{2,1,0:T(8,128)(2,1)} %bitcast.12), calls=%async_computation.1 | async-start | bytes 4718592 | tf_op jit(solution)/shard_map/rows/all_to_all | solution.py:15
  25.6 0.0 copy-done.1
  25.6 0.6 dynamic_slice.3
  26.2 0.5 broadcast.62
  26.7 0.7 reduce.3
  27.4 0.1 reshape.79
  27.5 2.6 %convert_reduce_fusion = s32[1536]{0:T(1024)S(1)} fusion(s32[1536]{0:T(1024)S(1)} %reshape.79), kind=kLoop, calls=%fused_computation | loop fusion | flops 11794944 | bytes 12288 | tf_op jit(solution)/shard_map/reduce_sum | solution.py:52
  30.1 0.1 convert_element_type.49
  30.2 0.7 broadcast_subtract_fusion
  30.8 0.4 convert_reduce_fusion.1
  31.3 49.9 %all-to-all-done.1 = bf16[32,48,768]{2,1,0:T(8,128)(2,1)S(1)} async-done(((bf16[32,48,768]{2,1,0:T(8,128)(2,1)}), bf16[32,48,768]{2,1,0:T(8,128)(2,1)S(1)}, u32[]{:S(2)}, u32[]{:S(2)}) %all-to-all-start.1) | async-done | bytes 2359328 | tf_op jit(solution)/shard_map/rows/all_to_all | solution.py:15
  81.2 1.8 %multiply_reduce_fusion = (f32[576]{0:T(1024)S(1)}, f32[576,768]{1,0:T(8,128)S(1)}) fusion(f32[576]{0:T(1024)S(1)} %broadcast_maximum_fusion, bf16[1536,768]{1,0:T(8,128)(2,1)S(1)} %bitcast.10, s32[1536]{0:T(1024)S(1)} %broadcast_subtract_fusion), kind=kOutput, calls=%fused_computation.16 | convolution fusion | flops 1361165824 | bytes 4139520 | tf_op jit(solution)/shard_map/dot_general | solution.py:56
  83.0 1.6 %select_reduce_fusion = f32[1536]{0:T(1024)S(1)} fusion(bf16[1536,768]{1,0:T(8,128)(2,1)S(1)} %bitcast.11, s32[1536]{0:T(1024)S(1)} %broadcast_subtract_fusion, f32[576,768]{1,0:T(8,128)S(1)} %get-tuple-element.12, f32[576]{0:T(1024)S(1)} %maximum_multiply_fusion), kind=kOutput, calls=%fused_computation.3 | convolution fusion | flops 1362491904 | bytes 4143360 | tf_op jit(solution)/shard_map/dot_general | solution.py:64
  84.6 0.0 copy-done
  84.6 0.1 sub.34
  84.7 0.7 pad_maximum_fusion
  85.4 3.3 %all-to-all-start.2 = ((f32[32,1,96]{2,1,0:T(1,128)}), f32[32,1,96]{2,1,0:T(1,128)S(1)}, u32[]{:S(2)}, u32[]{:S(2)}) async-start(f32[32,1,96]{2,1,0:T(1,128)} %bitcast.3), calls=%async_computation.2 | async-start | bytes 32768 | tf_op jit(solution)/shard_map/all_to_all | solution.py:15
  88.7 2.6 %fusion.13 = bf16[1,576,768]{2,1,0:T(8,128)(2,1)} fusion(f32[576,768]{1,0:T(8,128)} %copy-done, f32[576]{0:T(1024)S(1)} %maximum_multiply_fusion), kind=kLoop, calls=%fused_computation.37 | loop fusion | flops 884736 | bytes 2656512 | tf_op jit(solution)/shard_map/broadcast_in_dim | solution.py:81
  91.2 4.6 %all-to-all-done.2 = f32[32,1,96]{2,1,0:T(1,128)S(1)} async-done(((f32[32,1,96]{2,1,0:T(1,128)}), f32[32,1,96]{2,1,0:T(1,128)S(1)}, u32[]{:S(2)}, u32[]{:S(2)}) %all-to-all-start.2) | async-done | bytes 12320 | tf_op jit(solution)/shard_map/all_to_all | solution.py:15
  95.8 0.1 fusion.9
  95.9 0.1 broadcast_in_dim.65
  96.0 0.1 broadcast_in_dim.62
  96.0 1.6 %select_reduce_fusion.1 = (f32[512]{0:T(512)S(1)}, f32[512]{0:T(512)}) fusion(f32[1536]{0:T(1024)S(1)} %broadcast_in_dim.65, s32[512]{0:T(512)S(1)} %get-tuple-element.13, f32[1536]{0:T(1024)S(1)} %broadcast_in_dim.62), kind=kLoop, calls=%fused_computation.8 | loop fusion | flops 3931136 | bytes 18432 | tf_op jit(solution)/shard_map/reduce_sum | solution.py:78
  97.7 0.6 convert_element_type.50
  (9 shorter events, 0.0 us)
Async XLA Ops:
  22.7 2.9 %copy-start.1 = (s32[32]{0:T(128)S(1)}, s32[32]{0:T(128)}, u32[]{:S(2)}) copy-start(s32[32]{0:T(128)} %param.5) | copy-start | bytes 388
  22.7 58.5 %all-to-all-start.1 = ((bf16[32,48,768]{2,1,0:T(8,128)(2,1)}), bf16[32,48,768]{2,1,0:T(8,128)(2,1)S(1)}, u32[]{:S(2)}, u32[]{:S(2)}) async-start(bf16[32,48,768]{2,1,0:T(8,128)(2,1)} %bitcast.12), calls=%async_computation.1 | async-start | bytes 4718592 | tf_op jit(solution)/shard_map/rows/all_to_all | solution.py:15
  82.9 1.7 %copy-start = (f32[576,768]{1,0:T(8,128)}, f32[576,768]{1,0:T(8,128)S(1)}, u32[]{:S(2)}) copy-start(f32[576,768]{1,0:T(8,128)S(1)} %get-tuple-element.12) | copy-start | bytes 5308420
  85.4 10.4 %all-to-all-start.2 = ((f32[32,1,96]{2,1,0:T(1,128)}), f32[32,1,96]{2,1,0:T(1,128)S(1)}, u32[]{:S(2)}, u32[]{:S(2)}) async-start(f32[32,1,96]{2,1,0:T(1,128)} %bitcast.3), calls=%async_computation.2 | async-start | bytes 32768 | tf_op jit(solution)/shard_map/all_to_all | solution.py:15

commit v3 on v2

--- a/solution.py
+++ b/solution.py
@@ -32,7 +32,6 @@
     earlier = (owner_of[:, None] == owner_of[None, :]) & (row_range[None, :] < row_range[:, None])
     target = owner_of * slot_count + jnp.sum(earlier, axis=1, dtype=jnp.int32)
     placed = place_range[:, None] == target[None, :]
-    send_ids = jnp.sum(jnp.where(placed, cluster_ids[None, :] + 1, 0), axis=1, dtype=jnp.int32) - 1
     values = embeddings.astype(jnp.float32)
     unit_rows = (
         values * lax.rsqrt(jnp.sum(values * values, axis=1, keepdims=True) + epsilon)
@@ -40,16 +39,42 @@
     send_rows = jnp.dot(
         placed.astype(jnp.bfloat16), unit_rows, preferred_element_type=jnp.float32
     ).astype(jnp.bfloat16)
-    send_rows, send_ids = lax.optimization_barrier((send_rows, send_ids))
+    send_rows, own_ids = lax.optimization_barrier((send_rows, cluster_ids))
     with jax.named_scope("rows"):
         flat_rows = exchange(send_rows.reshape(owner_total, slot_count, feature_count)).reshape(
             places, feature_count
         )
     with jax.named_scope("ids"):
-        flat_ids = exchange(send_ids.reshape(owner_total, slot_count)).reshape(-1)
+        every_id = lax.all_gather(own_ids, axes, tiled=False)
 
-    twins = (flat_ids[:, None] == flat_ids[None, :]) & (place_range[None, :] < place_range[:, None])
-    rank = jnp.sum(twins, axis=1, dtype=jnp.int32)
+    flat_every = every_id.reshape(1, -1)
+    every_range = jnp.arange(owner_total * row_count, dtype=jnp.int32)[None, :]
+    local_slot = jnp.sum(
+        (flat_every == cluster_ids[:, None])
+        & (every_range < (position * row_count + row_range)[:, None]),
+        axis=1,
+        dtype=jnp.int32,
+    )
+    first = owner_bounds[position]
+    beyond = jnp.sum(jnp.where(jnp.arange(owner_total) == position + 1, owner_bounds, 0))
+    beyond = jnp.where(position + 1 < owner_total, beyond, CL_DEV * owner_total)
+    owned = (every_id >= first) & (every_id < beyond)
+    upper = (row_range[:, None] < row_range[None, :]).astype(jnp.bfloat16)
+    place_in = jnp.dot(
+        owned.astype(jnp.bfloat16), upper, preferred_element_type=jnp.float32
+    ).astype(jnp.int32)
+    place_in = jnp.where(owned, place_in, -1)
+    slot_range = jnp.arange(slot_count, dtype=jnp.int32)
+    flat_ids = (
+        jnp.sum(
+            jnp.where(
+                place_in[:, None, :] == slot_range[None, :, None], every_id[:, None, :] + 1, 0
+            ),
+            axis=2,
+            dtype=jnp.int32,
+        ).reshape(-1)
+        - 1
+    )
     local_index = flat_ids - owner_bounds[position]
     membership = jnp.arange(owner_limit, dtype=jnp.int32)[:, None] == local_index[None, :]
     members = jnp.sum(membership, axis=1, dtype=jnp.float32)
@@ -65,19 +90,9 @@
         unit_centroid, flat_rows, (((1,), (1,)), ((), ())), preferred_element_type=jnp.float32
     )
     owner_distance = 1.0 - jnp.sum(jnp.where(membership, products, 0.0), axis=0)
-    answers = jnp.concatenate(
-        [
-            owner_distance.reshape(owner_total, slot_count),
-            rank.astype(jnp.float32).reshape(owner_total, slot_count),
-        ],
-        axis=1,
-    )
-    returned = exchange(answers)
+    returned = exchange(owner_distance.reshape(owner_total, slot_count)).reshape(1, -1)
     mine = target[:, None] == place_range[None, :]
-    distance = jnp.sum(jnp.where(mine, returned[:, :slot_count].reshape(1, -1), 0.0), axis=1)
-    local_slot = jnp.sum(
-        jnp.where(mine, returned[:, slot_count:].reshape(1, -1), 0.0), axis=1
-    ).astype(jnp.int32)
+    distance = jnp.sum(jnp.where(mine, returned, 0.0), axis=1)
     return (distance, local_slot, unit_centroid[None])
 
 

time: 98.6 us -> 153 us (1.55)
  blocking collectives: 14.3 us -> 110 us
  waiting for transfers between devices: 54.5 us -> 4.58 us
  other arithmetic: 13.4 us -> 17.3 us
  starting transfers between devices: 6.19 us -> 9.84 us
    all_gather x0 -> x1, blocking collectives: none -> 110 us  [shards(): every_id = lax.all_gather(own_ids, axes, tiled=False)]
    all_to_all x2, waiting for transfers between devices: 54.5 us -> 4.58 us  [exchange(): return lax.all_to_all(part, axes, split_axis=0, concat_axis=0, tiled=True)]
    all_to_all x1 -> x0, blocking collectives: 14.3 us -> none  [exchange(): return lax.all_to_all(part, axes, split_axis=0, concat_axis=0, tiled=True)]
    reduce_sum x3 -> x4, other arithmetic: 4.68 us -> 9.83 us  [the longest x1 7.51 us: shards(): jnp.sum((flat_every == cluster_ids[:, None]) & (every_range < (position *...]
    all_to_all x2, starting transfers between devices: 6.19 us -> 9.84 us  [exchange(): return lax.all_to_all(part, axes, split_axis=0, concat_axis=0, tiled=True)]
  transfers between devices with their start and end apart: 2 -> 2, of which waited for: 2 -> 1; matrix products, arithmetic and copies ran while one was open for 8% -> 9% of each run, Pallas kernels for 0% -> 0%
where the time goes in v3:
time: 153 us
  blocking collectives  110 us (72%)
  other arithmetic  17.3 us (11%)
  starting transfers between devices  9.84 us (6%)
  matrix products  7.71 us (5%)
  waiting for transfers between devices  4.58 us (3%)
  local copies, waits for them, and re-layouts  1.99 us (1%)
    all_gather x1, blocking collectives, shards(): every_id = lax.all_gather(own_ids, axes, tiled=False)  110 us
    all_to_all x2, starting transfers between devices, exchange(): return lax.all_to_all(part, axes, split_axis=0, concat_axis=0, tiled=True)  9.84 us
    reduce_sum x1, other arithmetic, shards(): jnp.sum((flat_every == cluster_ids[:, None]) & (every_range < (position *...  7.51 us
    all_to_all x2, waiting for transfers between devices, exchange(): return lax.all_to_all(part, axes, split_axis=0, concat_axis=0, tiled=True)  4.58 us
    dot_general x1, matrix products, shards(): jnp.dot(placed.astype(jnp.bfloat16), unit_rows, preferred_element_type=jn...  4.15 us
  transfers between devices with their start and end apart: 2, of which 1 were waited for; matrix products, arithmetic and copies ran while one was open for 9% of the time, Pallas kernels for 0%

profile of v3, /device:TPU:0, one launch (start us, length us, event | category | flops | bytes accessed | tf_op | source)
XLA Modules:
  0.0 152.6 jit_solution(11563294432657460733)
XLA Ops:
  0.6 0.8 convert_reduce_fusion.3
  1.4 0.3 convert_reduce_fusion.2
  1.7 1.4 fusion.3
  3.0 4.1 %convolution_convert_fusion = bf16[1536,768]{1,0:T(8,128)(2,1)} fusion(s32[512]{0:T(512)S(1)} %multiply_add_fusion, bf16[512,768]{1,0:T(8,128)(2,1)} %param.3, f32[512]{0:T(512)S(1)} %add_rsqrt_fusion), kind=kOutput, calls=%fused_computation.7 | convolution fusion | flops 1211105280 | bytes 3149824 | tf_op jit(solution)/shard_map/dot_general | solution.py:39
  7.2 0.0 copy-start.1
  7.2 0.0 copy-start.2
  7.2 7.3 %all-to-all-start = ((bf16[32,48,768]{2,1,0:T(8,128)(2,1)}), bf16[32,48,768]{2,1,0:T(8,128)(2,1)S(1)}, u32[]{:S(2)}, u32[]{:S(2)}) async-start(bf16[32,48,768]{2,1,0:T(8,128)(2,1)} %bitcast.13), calls=%async_computation | async-start | bytes 4718592 | tf_op jit(solution)/shard_map/rows/all_to_all | solution.py:15
  14.5 0.0 copy-done.1
  14.5 109.7 %all-gather.1 = s32[32,1,512]{2,1,0:T(1,128)S(1)} all-gather(s32[1,1,512]{2,1,0:T(1,128)S(1)} %bitcast.17), channel_id=2, replica_groups=mesh['grp'=4,'rep'=8] {'grp','rep'}, dimensions={0}, use_global_device_ids=true | all-gather | bytes 67584 | tf_op jit(solution)/shard_map/ids/all_gather | solution.py:48
  124.3 0.0 copy-done.2
  124.3 0.6 dynamic_slice.4
  124.9 0.6 fusion.10
  126.2 0.7 compare_and_fusion
  126.9 0.2 fusion.6
  127.1 0.6 select_reduce_fusion.2
  127.7 0.7 add_subtract_fusion
  128.4 0.1 sub.43
  128.5 0.4 convert_reduce_fusion.1
  128.9 7.5 %convert_reduce_fusion = s32[512]{0:T(512)} fusion(s32[16384]{0:T(1024)S(1)} %bitcast.16, s32[512]{0:T(512)S(1)} %iota_add_fusion, s32[512]{0:T(512)S(1)} %copy-done.1), kind=kLoop, calls=%fused_computation | loop fusion | flops 41942528 | bytes 71680 | tf_op jit(solution)/shard_map/reduce_sum | solution.py:52
  136.4 0.0 all-to-all-done
  136.4 1.8 %multiply_reduce_fusion = (f32[576]{0:T(1024)S(1)}, f32[576,768]{1,0:T(8,128)S(1)}) fusion(f32[576]{0:T(1024)S(1)} %broadcast_maximum_fusion, bf16[1536,768]{1,0:T(8,128)(2,1)S(1)} %bitcast.11, s32[1536]{0:T(1024)S(1)} %sub.43), kind=kOutput, calls=%fused_computation.16 | convolution fusion | flops 1361165824 | bytes 4139520 | tf_op jit(solution)/shard_map/dot_general | solution.py:81
  138.2 0.0 copy-start
  138.2 1.6 %select_reduce_fusion = f32[1536]{0:T(1024)S(1)} fusion(bf16[1536,768]{1,0:T(8,128)(2,1)S(1)} %bitcast.12, s32[1536]{0:T(1024)S(1)} %sub.43, f32[576,768]{1,0:T(8,128)S(1)} %get-tuple-element.8, f32[576]{0:T(1024)S(1)} %maximum_multiply_fusion), kind=kOutput, calls=%fused_computation.3 | convolution fusion | flops 1362491904 | bytes 4143360 | tf_op jit(solution)/shard_map/dot_general | solution.py:89
  139.8 0.0 copy-done
  139.9 0.7 sub.45
  140.6 2.5 %all-to-all-start.1 = ((f32[32,1,48]{2,1,0:T(1,128)}), f32[32,1,48]{2,1,0:T(1,128)S(1)}, u32[]{:S(2)}, u32[]{:S(2)}) async-start(f32[32,1,48]{2,1,0:T(1,128)} %sub.45), calls=%async_computation.1 | async-start | bytes 32768 | tf_op jit(solution)/shard_map/all_to_all | solution.py:15
  143.1 2.6 %fusion.15 = bf16[1,576,768]{2,1,0:T(8,128)(2,1)} fusion(f32[576,768]{1,0:T(8,128)} %copy-done, f32[576]{0:T(1024)S(1)} %maximum_multiply_fusion), kind=kLoop, calls=%fused_computation.41 | loop fusion | flops 884736 | bytes 2656512 | tf_op jit(solution)/shard_map/broadcast_in_dim | solution.py:96
  145.6 4.6 %all-to-all-done.1 = f32[32,1,48]{2,1,0:T(1,128)S(1)} async-done(((f32[32,1,48]{2,1,0:T(1,128)}), f32[32,1,48]{2,1,0:T(1,128)S(1)}, u32[]{:S(2)}, u32[]{:S(2)}) %all-to-all-start.1) | async-done | bytes 6176 | tf_op jit(solution)/shard_map/all_to_all | solution.py:15
  150.2 0.5 broadcast.92
  150.7 0.7 reduce.3
  151.4 0.1 broadcast_in_dim.45
  151.5 1.1 select_reduce_fusion.1
  (10 shorter events, 0.1 us)
Async XLA Ops:
  7.2 7.3 %copy-start.1 = (s32[512]{0:T(512)S(1)}, s32[512]{0:T(512)}, u32[]{:S(2)}) copy-start(s32[512]{0:T(512)} %param.4) | copy-start | bytes 6148
  7.2 117.1 %copy-start.2 = (s32[32]{0:T(128)S(1)}, s32[32]{0:T(128)}, u32[]{:S(2)}) copy-start(s32[32]{0:T(128)} %param.5) | copy-start | bytes 388
  7.2 129.2 %all-to-all-start = ((bf16[32,48,768]{2,1,0:T(8,128)(2,1)}), bf16[32,48,768]{2,1,0:T(8,128)(2,1)S(1)}, u32[]{:S(2)}, u32[]{:S(2)}) async-start(bf16[32,48,768]{2,1,0:T(8,128)(2,1)} %bitcast.13), calls=%async_computation | async-start | bytes 4718592 | tf_op jit(solution)/shard_map/rows/all_to_all | solution.py:15
  138.2 1.6 %copy-start = (f32[576,768]{1,0:T(8,128)}, f32[576,768]{1,0:T(8,128)S(1)}, u32[]{:S(2)}) copy-start(f32[576,768]{1,0:T(8,128)S(1)} %get-tuple-element.8) | copy-start | bytes 5308420
  140.6 9.7 %all-to-all-start.1 = ((f32[32,1,48]{2,1,0:T(1,128)}), f32[32,1,48]{2,1,0:T(1,128)S(1)}, u32[]{:S(2)}, u32[]{:S(2)}) async-start(f32[32,1,48]{2,1,0:T(1,128)} %sub.45), calls=%async_computation.1 | async-start | bytes 32768 | tf_op jit(solution)/shard_map/all_to_all | solution.py:15

commit v4 on v1

--- a/solution.py
+++ b/solution.py
@@ -32,7 +32,7 @@
     earlier = (owner_of[:, None] == owner_of[None, :]) & (row_range[None, :] < row_range[:, None])
     target = owner_of * slot_count + jnp.sum(earlier, axis=1, dtype=jnp.int32)
     placed = place_range[:, None] == target[None, :]
-    send_ids = jnp.sum(jnp.where(placed, cluster_ids[None, :] + 1, 0), axis=1, dtype=jnp.int32) - 1
+    send_ids = jnp.sum(jnp.where(placed, cluster_ids[None, :] + 1, 0), axis=1, dtype=jnp.int32)
     flat_ids = exchange(send_ids.reshape(owner_total, slot_count)).reshape(-1)
 
     values = embeddings.astype(jnp.float32)
@@ -48,7 +48,7 @@
 
     twins = (flat_ids[:, None] == flat_ids[None, :]) & (place_range[None, :] < place_range[:, None])
     rank = jnp.sum(twins, axis=1, dtype=jnp.int32)
-    local_index = flat_ids - owner_bounds[position]
+    local_index = flat_ids - (owner_bounds[position] + 1)
     membership = jnp.arange(owner_limit, dtype=jnp.int32)[:, None] == local_index[None, :]
     members = jnp.sum(membership, axis=1, dtype=jnp.float32)
     member_sums = jnp.dot(
@@ -73,9 +73,8 @@
     returned = exchange(answers)
     mine = target[:, None] == place_range[None, :]
     distance = jnp.sum(jnp.where(mine, returned[:, :slot_count].reshape(1, -1), 0.0), axis=1)
-    local_slot = jnp.sum(
-        jnp.where(mine, returned[:, slot_count:].reshape(1, -1), 0.0), axis=1
-    ).astype(jnp.int32)
+    ranks = returned[:, slot_count:].astype(jnp.int32).reshape(1, -1)
+    local_slot = jnp.sum(jnp.where(mine, ranks, 0), axis=1, dtype=jnp.int32)
     return (distance, local_slot, unit_centroid[None])
 
 

time: 95.1 us -> 95.1 us (level)
    reduce_sum x1 -> x2, other arithmetic: 1.63 us -> 2.19 us  [the longest x1 1.13 us: shards(): local_slot = jnp.sum(jnp.where(mine, ranks, 0), axis=1, dtype=jnp.int32)]
  transfers between devices with their start and end apart: 3 -> 3, of which waited for: 3 -> 3; matrix products, arithmetic and copies ran while one was open for 15% -> 14% of each run, Pallas kernels for 0% -> 0%
where the time goes in v4:
time: 95.1 us; the launch traced here: 94.6 us
  waiting for transfers between devices  56 us (59%)
  starting transfers between devices  14.7 us (15%)
  other arithmetic  12.8 us (13%)
  matrix products  7.53 us (8%)
  local copies, waits for them, and re-layouts  2.18 us (2%)
  between operations  1.39 us (1%)
    all_to_all x3, waiting for transfers between devices, exchange(): return lax.all_to_all(part, axes, split_axis=0, concat_axis=0, tiled=True)  56 us
    all_to_all x3, starting transfers between devices, exchange(): return lax.all_to_all(part, axes, split_axis=0, concat_axis=0, tiled=True)  14.7 us
    dot_general x1, matrix products, shards(): jnp.dot(placed.astype(jnp.bfloat16), unit_rows, preferred_element_type=jn...  4.14 us
    reduce_sum x1, other arithmetic, shards(): rank = jnp.sum(twins, axis=1, dtype=jnp.int32)  2.65 us
    broadcast_in_dim x1, other arithmetic, shards(): return (distance, local_slot, unit_centroid[None])  2.56 us
  transfers between devices with their start and end apart: 3, of which 3 were waited for; matrix products, arithmetic and copies ran while one was open for 14% of the time, Pallas kernels for 0%

profile of v4, /device:TPU:0, one launch (start us, length us, event | category | flops | bytes accessed | tf_op | source)
XLA Modules:
  0.0 94.6 jit_solution(5239430933378923763)
XLA Ops:
  0.6 0.8 convert_reduce_fusion.3
  1.4 0.3 convert_reduce_fusion.2
  1.7 0.7 multiply_add_fusion
  2.4 0.4 select_reduce_fusion.3
  2.8 0.7 all_to_all.17
  3.5 7.3 %all-to-all-start = ((s32[32,1,48]{2,1,0:T(1,128)}), s32[32,1,48]{2,1,0:T(1,128)S(1)}, u32[]{:S(2)}, u32[]{:S(2)}) async-start(s32[32,1,48]{2,1,0:T(1,128)} %all_to_all.17), calls=%async_computation | async-start | bytes 32768 | tf_op jit(solution)/shard_map/all_to_all | solution.py:15
  10.8 1.4 %fusion.3 = f32[512]{0:T(512)S(1)} fusion(bf16[512,768]{1,0:T(8,128)(2,1)} %param.3), kind=kLoop, calls=%fused_computation.18 | loop fusion | flops 1179136 | bytes 788480 | tf_op jit(solution)/shard_map/reduce_sum | solution.py:40
  12.2 4.1 %convolution_convert_fusion = bf16[1536,768]{1,0:T(8,128)(2,1)} fusion(s32[512]{0:T(512)S(1)} %get-tuple-element.7, bf16[512,768]{1,0:T(8,128)(2,1)} %param.3, f32[512]{0:T(512)S(1)} %add_rsqrt_fusion), kind=kOutput, calls=%fused_computation.7 | convolution fusion | flops 1211105280 | bytes 3149824 | tf_op jit(solution)/shard_map/dot_general | solution.py:42
  16.3 1.6 %all-to-all-done = s32[32,1,48]{2,1,0:T(1,128)S(1)} async-done(((s32[32,1,48]{2,1,0:T(1,128)}), s32[32,1,48]{2,1,0:T(1,128)S(1)}, u32[]{:S(2)}, u32[]{:S(2)}) %all-to-all-start) | async-done | bytes 6176 | tf_op jit(solution)/shard_map/all_to_all | solution.py:15
  17.9 4.3 %all-to-all-start.1 = ((bf16[32,48,768]{2,1,0:T(8,128)(2,1)}), bf16[32,48,768]{2,1,0:T(8,128)(2,1)S(1)}, u32[]{:S(2)}, u32[]{:S(2)}) async-start(bf16[32,48,768]{2,1,0:T(8,128)(2,1)} %bitcast.12), calls=%async_computation.1 | async-start | bytes 4718592 | tf_op jit(solution)/shard_map/all_to_all | solution.py:15
  22.2 0.0 copy-done.1
  22.2 0.6 dynamic_slice.3
  23.4 0.5 broadcast.57
  23.9 0.7 reduce.3
  24.6 0.1 reshape.79
  24.7 2.6 %convert_reduce_fusion = s32[1536]{0:T(1024)S(1)} fusion(s32[1536]{0:T(1024)S(1)} %reshape.79), kind=kLoop, calls=%fused_computation | loop fusion | flops 11794944 | bytes 12288 | tf_op jit(solution)/shard_map/reduce_sum | solution.py:50
  27.4 0.1 convert_element_type.49
  27.4 0.4 convert_reduce_fusion.1
  27.9 49.9 %all-to-all-done.1 = bf16[32,48,768]{2,1,0:T(8,128)(2,1)S(1)} async-done(((bf16[32,48,768]{2,1,0:T(8,128)(2,1)}), bf16[32,48,768]{2,1,0:T(8,128)(2,1)S(1)}, u32[]{:S(2)}, u32[]{:S(2)}) %all-to-all-start.1) | async-done | bytes 2359328 | tf_op jit(solution)/shard_map/all_to_all | solution.py:15
  77.8 1.8 %multiply_reduce_fusion = (f32[576]{0:T(1024)S(1)}, f32[576,768]{1,0:T(8,128)S(1)}) fusion(f32[576]{0:T(1024)S(1)} %broadcast_maximum_fusion, bf16[1536,768]{1,0:T(8,128)(2,1)S(1)} %bitcast.10, s32[1536]{0:T(1024)S(1)} %broadcast_subtract_fusion), kind=kOutput, calls=%fused_computation.16 | convolution fusion | flops 1361165824 | bytes 4139520 | tf_op jit(solution)/shard_map/dot_general | solution.py:54
  79.5 1.6 %select_reduce_fusion = f32[1536]{0:T(1024)S(1)} fusion(bf16[1536,768]{1,0:T(8,128)(2,1)S(1)} %bitcast.11, s32[1536]{0:T(1024)S(1)} %broadcast_subtract_fusion, f32[576,768]{1,0:T(8,128)S(1)} %get-tuple-element.6, f32[576]{0:T(1024)S(1)} %maximum_multiply_fusion), kind=kOutput, calls=%fused_computation.3 | convolution fusion | flops 1362491904 | bytes 4143360 | tf_op jit(solution)/shard_map/dot_general | solution.py:62
  81.2 0.0 copy-done
  81.2 0.1 sub.29
  81.3 0.7 pad_maximum_fusion
  82.0 3.1 %all-to-all-start.2 = ((f32[32,1,96]{2,1,0:T(1,128)}), f32[32,1,96]{2,1,0:T(1,128)S(1)}, u32[]{:S(2)}, u32[]{:S(2)}) async-start(f32[32,1,96]{2,1,0:T(1,128)} %bitcast.3), calls=%async_computation.2 | async-start | bytes 32768 | tf_op jit(solution)/shard_map/all_to_all | solution.py:15
  85.1 2.6 %fusion.12 = bf16[1,576,768]{2,1,0:T(8,128)(2,1)} fusion(f32[576,768]{1,0:T(8,128)} %copy-done, f32[576]{0:T(1024)S(1)} %maximum_multiply_fusion), kind=kLoop, calls=%fused_computation.36 | loop fusion | flops 884736 | bytes 2656512 | tf_op jit(solution)/shard_map/broadcast_in_dim | solution.py:78
  87.6 4.6 %all-to-all-done.2 = f32[32,1,96]{2,1,0:T(1,128)S(1)} async-done(((f32[32,1,96]{2,1,0:T(1,128)}), f32[32,1,96]{2,1,0:T(1,128)S(1)}, u32[]{:S(2)}, u32[]{:S(2)}) %all-to-all-start.2) | async-done | bytes 12320 | tf_op jit(solution)/shard_map/all_to_all | solution.py:15
  92.2 0.1 slice_convert_fusion
  92.3 0.1 broadcast_in_dim.68
  92.4 1.1 %select_reduce_fusion.2 = f32[512]{0:T(512)} fusion(f32[1536]{0:T(1024)S(1)} %broadcast_in_dim.68, s32[512]{0:T(512)S(1)} %get-tuple-element.7), kind=kLoop, calls=%fused_computation.9 | loop fusion | flops 2358784 | bytes 10240 | tf_op jit(solution)/shard_map/reduce_sum | solution.py:75
  93.4 0.1 broadcast_in_dim.71
  93.5 1.1 %select_reduce_fusion.1 = s32[512]{0:T(512)} fusion(s32[1536]{0:T(1024)S(1)} %broadcast_in_dim.71, s32[512]{0:T(512)S(1)} %get-tuple-element.7), kind=kLoop, calls=%fused_computation.8 | loop fusion | flops 2358784 | bytes 10240 | tf_op jit(solution)/shard_map/reduce_sum | solution.py:77
  (9 shorter events, 0.0 us)
Async XLA Ops:
  3.5 14.4 %all-to-all-start = ((s32[32,1,48]{2,1,0:T(1,128)}), s32[32,1,48]{2,1,0:T(1,128)S(1)}, u32[]{:S(2)}, u32[]{:S(2)}) async-start(s32[32,1,48]{2,1,0:T(1,128)} %all_to_all.17), calls=%async_computation | async-start | bytes 32768 | tf_op jit(solution)/shard_map/all_to_all | solution.py:15
  17.9 4.3 %copy-start.1 = (s32[32]{0:T(128)S(1)}, s32[32]{0:T(128)}, u32[]{:S(2)}) copy-start(s32[32]{0:T(128)} %param.5) | copy-start | bytes 388
  17.9 59.9 %all-to-all-start.1 = ((bf16[32,48,768]{2,1,0:T(8,128)(2,1)}), bf16[32,48,768]{2,1,0:T(8,128)(2,1)S(1)}, u32[]{:S(2)}, u32[]{:S(2)}) async-start(bf16[32,48,768]{2,1,0:T(8,128)(2,1)} %bitcast.12), calls=%async_computation.1 | async-start | bytes 4718592 | tf_op jit(solution)/shard_map/all_to_all | solution.py:15
  79.5 1.7 %copy-start = (f32[576,768]{1,0:T(8,128)}, f32[576,768]{1,0:T(8,128)S(1)}, u32[]{:S(2)}) copy-start(f32[576,768]{1,0:T(8,128)S(1)} %get-tuple-element.6) | copy-start | bytes 5308420
  82.0 10.3 %all-to-all-start.2 = ((f32[32,1,96]{2,1,0:T(1,128)}), f32[32,1,96]{2,1,0:T(1,128)S(1)}, u32[]{:S(2)}, u32[]{:S(2)}) async-start(f32[32,1,96]{2,1,0:T(1,128)} %bitcast.3), calls=%async_computation.2 | async-start | bytes 32768 | tf_op jit(solution)/shard_map/all_to_all | solution.py:15
